TPU v7x, 32 devices: a whole 2x2x4 slice. The times are simulated.
32 devices in a mesh: grp: 2 (over y), gy: 4 (over z), gx: 2 (over x), gz: 2 (over core).
Axes of the slice: x: 2, y: 2, z: 4, core: 2. Of those that a mesh axis runs over, the one named last changes fastest.
Arguments:
- pair: bfloat16 [1024, 512, 128], P(('grp', 'gx', 'gz'), 'gy'), parts along dimension 0, may hold values from -6 to 6
- lengths: int32 [2], P('grp'), parts along dimension 0, may hold values from 256 to 512
- ln_gain: float32 [128], replicated, may hold values from 0.1 to 1.9
- ln_bias: float32 [128], replicated, may hold values from -3 to 3
- w_ab: bfloat16 [128, 512], replicated, may hold values from -0.5 to 0.5
- w_gate: bfloat16 [128, 128], replicated, may hold values from -0.5 to 0.5
- out_gain: float32 [128], replicated, may hold values from 0.1 to 1.9
- out_bias: float32 [128], replicated, may hold values from -3 to 3
- w_out: bfloat16 [128, 128], replicated, may hold values from -0.5 to 0.5
Outputs:
- update: bfloat16 [1024, 512, 128], P(('grp', 'gx', 'gz'), 'gy'), parts along dimension 0
There are 2 independent parts, one for each index of `grp`. A program takes and returns all parts, laid end to end along the dimension named above; an argument that names none is the same for every part. Nothing has to cross between parts.
Inputs may be any that keep to these rules, and one draw needn't show every extreme that they name: Residues from lengths[0] on are padding.
All inputs are finite; a program needn't handle non-finite values.
Results may differ from a plain program's by a relative error of at most 0.0052.
Values may be sent and summed in bfloat16 or wider, within the bound.
A program may use at most 128 MiB of HBM per device.

v0:
```python
import jax
import jax.numpy as jnp
from jax import lax
from jax.sharding import PartitionSpec as P


def layer_norm(values, gain, bias):
    values = values.astype(jnp.float32)
    mean = jnp.mean(values, -1, keepdims=True)
    spread = jnp.mean(jnp.square(values - mean), -1, keepdims=True)
    return (values - mean) * lax.rsqrt(spread + 1e-05) * gain + bias


def channel_norm(values, gain, bias):
    mean = jnp.mean(values, 0, keepdims=True)
    spread = jnp.mean(jnp.square(values - mean), 0, keepdims=True)
    return (values - mean) * lax.rsqrt(spread + 1e-05) * gain[:, None, None] + bias[:, None, None]


def body(pair, lengths, ln_gain, ln_bias, w_ab, w_gate, out_gain, out_bias, w_out):
    tile_rows, tile_cols, width = pair.shape
    hidden = w_out.shape[0]
    row_start = lax.axis_index(("gx", "gz")) * tile_rows
    col_index = lax.axis_index("gy")
    col_start = col_index * tile_cols
    normed = layer_norm(pair, ln_gain, ln_bias).astype(jnp.bfloat16)
    flat = normed.reshape(tile_rows * tile_cols, width)
    proj = jnp.dot(flat, w_ab, preferred_element_type=jnp.float32).reshape(
        tile_rows, tile_cols, 4 * hidden
    )
    row_live = (row_start + jnp.arange(tile_rows, dtype=jnp.int32) < lengths[0]).astype(jnp.float32)
    col_live = (col_start + jnp.arange(tile_cols, dtype=jnp.int32) < lengths[0]).astype(jnp.float32)
    pair_mask = (row_live[:, None] * col_live[None, :])[..., None]
    left = (pair_mask * jax.nn.sigmoid(proj[..., :hidden]) * proj[..., hidden : 2 * hidden]).astype(
        jnp.bfloat16
    )
    right = (
        pair_mask * jax.nn.sigmoid(proj[..., 2 * hidden : 3 * hidden]) * proj[..., 3 * hidden :]
    ).astype(jnp.bfloat16)
    left_major = jnp.transpose(left, (2, 0, 1))
    right_major = jnp.transpose(right, (2, 0, 1))
    column_rows = lax.all_gather(right_major, ("gx", "gz"), axis=1, tiled=True)
    right_mine = lax.all_to_all(column_rows, "gy", split_axis=1, concat_axis=2, tiled=True)
    triangle = jnp.einsum(
        "cik,cjk->cij",
        lax.all_gather(left_major, "gy", axis=2, tiled=True),
        right_mine,
        preferred_element_type=jnp.float32,
    )
    tri_norm = channel_norm(triangle, out_gain, out_bias).astype(jnp.bfloat16)
    gate = jax.nn.sigmoid(jnp.dot(flat, w_gate, preferred_element_type=jnp.float32)).reshape(
        tile_rows, tile_cols, width
    )
    projected = jnp.einsum("cij,cd->ijd", tri_norm, w_out, preferred_element_type=jnp.float32)
    return (gate * projected).astype(jnp.bfloat16)


def solution(mesh):
    in_specs = (P(("grp", "gx", "gz"), "gy", None), P("grp"), P(), P(), P(), P(), P(), P(), P())
    out_specs = P(("grp", "gx", "gz"), "gy", None)
    return jax.shard_map(body, mesh=mesh, in_specs=in_specs, out_specs=out_specs, check_vma=False)
```

profile of v0, /device:TPU:0, one launch (start us, length us, event | category | flops | bytes accessed | tf_op | source)
XLA Modules:
  0.0 898.8 jit_solution(9406988459465322010)
XLA Ops:
  6.5 0.0 copy-start
  6.5 0.0 copy-start.7
  6.5 0.0 copy-start.6
  6.5 0.0 all-gather.5.cloned.1.call-start
  6.6 0.0 copy-start.3
  7.4 3.8 convert_reduce_fusion
  11.2 6.0 fusion.5
  17.2 0.1 broadcast_multiply_fusion
  17.3 0.0 copy-done.7
  17.3 0.0 copy-done.6
  17.3 0.0 copy-done.3
  17.4 4.9 fusion.8
  22.3 0.0 copy-done
  22.3 0.0 copy-start.4
  22.3 13.1 %fusion.25 = f32[128,128,512]{2,1,0:T(8,128)} fusion(bf16[128,128,128]{2,1,0:T(8,128)(2,1)S(1)} %fusion.8, bf16[128,512]{1,0:T(8,128)(2,1)S(1)} %copy-done), kind=kOutput, calls=%fused_computation.34 | convolution fusion | flops 2147483648 | bytes 37879808 | tf_op jit(solution)/shard_map/dot_general | solution.py:28
  35.5 0.0 copy-done.4
  35.5 15.6 %fusion.22 = (bf16[128,128,128]{0,2,1:T(8,128)(2,1)}, bf16[128,128,128]{0,2,1:T(8,128)(2,1)}) fusion(f32[128,128,512]{2,1,0:T(8,128)} %fusion.25, f32[128,128]{1,0:T(8,128)S(1)} %broadcast_multiply_fusion), kind=kLoop, calls=%fused_computation.33 | loop fusion | flops 25165824 | bytes 42008576 | tf_op jit(solution)/shard_map/transpose | solution.py:41
  51.1 6.4 copy.13
  57.4 0.0 all-gather.5.cloned.1.call-update
  57.5 0.0 all-gather.3.cloned.1.call-start
  57.5 0.7 all-gather.3.cloned.1.call-update
  58.2 0.0 copy-start.10
  58.2 108.0 %all-gather.5.cloned.1.call-done = bf16[128,512,128]{2,0,1:T(8,128)(2,1)} async-done(((bf16[128,128,128]{2,0,1:T(8,128)(2,1)}), bf16[128,512,128]{2,0,1:T(8,128)(2,1)}) %all-gather.5.cloned.1.call-update) | async-done | bytes 16777232 | tf_op jit(solution)/shard_map/all_gather | solution.py:42
  166.2 7.3 all-to-all-start
  173.5 0.0 copy-done.10
  173.5 9.0 %fusion.2 = f32[16384,128]{1,0:T(8,128)} fusion(bf16[16384,128]{1,0:T(8,128)(2,1)} %bitcast.24, bf16[128,128]{1,0:T(8,128)(2,1)S(1)} %copy-done.10), kind=kOutput, calls=%fused_computation.3 | convolution fusion | flops 543162368 | bytes 12615680 | tf_op jit(solution)/shard_map/dot_general | solution.py:51
  182.5 580.3 %all-gather.3.cloned.1.call-done = bf16[128,128,512]{0,2,1:T(8,128)(2,1)} async-done(((bf16[128,128,128]{0,2,1:T(8,128)(2,1)}), bf16[128,128,512]{0,2,1:T(8,128)(2,1)}) %all-gather.3.cloned.1.call-update) | async-done | bytes 16777232 | tf_op jit(solution)/shard_map/all_gather | solution.py:46
  762.8 23.4 %copy.15 = bf16[128,128,512]{2,1,0:T(8,128)(2,1)} copy(bf16[128,128,512]{0,2,1:T(8,128)(2,1)} %all-gather.3.cloned.1.call-done) | data formatting | bytes 33554432 | tf_op jit(solution)/shard_map/all_gather | solution.py:46
  786.2 20.3 %all-to-all-done = bf16[128,512,128]{2,0,1:T(8,128)(2,1)} async-done(((bf16[128,512,128]{2,0,1:T(8,128)(2,1)}), bf16[128,512,128]{2,0,1:T(8,128)(2,1)}, u32[]{:S(2)}, u32[]{:S(2)}) %all-to-all-start) | async-done | bytes 16777248 | tf_op jit(solution)/shard_map/all_to_all | solution.py:43
  806.5 22.0 %copy.22 = bf16[128,4,128,128]{3,1,2,0:T(4,128)(2,1)} copy(bf16[128,4,128,128]{3,0,2,1:T(8,128)(2,1)} %bitcast.6) | data formatting | bytes 33554432 | tf_op jit(solution)/shard_map/all_to_all | solution.py:43
  828.6 24.9 %all_to_all.16 = bf16[128,128,512]{2,1,0:T(8,128)(2,1)} reshape(bf16[128,128,4,128]{3,2,1,0:T(4,128)(2,1)} %bitcast.23) | data formatting | bytes 33554432 | tf_op jit(solution)/shard_map/all_to_all | solution.py:43
  853.4 16.4 %fusion.28 = (f32[128,128]{1,0:T(8,128)S(1)}, f32[128,128,128]{2,1,0:T(8,128)}) fusion(bf16[128,128,512]{2,1,0:T(8,128)(2,1)} %copy.15, bf16[128,128,512]{2,1,0:T(8,128)(2,1)} %all_to_all.16), kind=kOutput, calls=%fused_computation.44 | convolution fusion | flops 2149564416 | bytes 42008576 | tf_op jit(solution)/shard_map/cik,cjk->cij/dot_general | solution.py:44
  869.8 0.0 copy-start.2
  869.8 0.0 copy-start.8
  869.8 0.0 copy-start.9
  869.8 4.4 multiply_reduce_fusion
  874.2 0.0 copy-start.5
  874.3 1.3 copy-done.2
  875.6 0.0 copy-done.8
  875.6 0.0 copy-done.9
  875.6 2.0 add_convert_fusion
  877.6 0.0 copy-start.1
  877.6 0.0 copy-done.5
  877.6 14.4 %multiply_convert_fusion = bf16[128,128,128]{2,1,0:T(8,128)(2,1)} fusion(f32[128,128,128]{2,1,0:T(8,128)} %bitcast.25, bf16[128,128,128]{2,1,0:T(8,128)(2,1)S(1)} %add_convert_fusion, bf16[128,128]{1,0:T(8,128)(2,1)S(1)} %copy-done.5), kind=kOutput, calls=%fused_computation.27 | convolution fusion | flops 541065216 | bytes 16809984 | tf_op jit(solution)/shard_map/cij,cd->ijd/dot_general | solution.py:54
  891.9 0.0 copy-done.1
  (5 shorter events, 0.1 us)
Async XLA Ops:
  6.5 15.8 %copy-start = (bf16[128,512]{1,0:T(8,128)(2,1)S(1)}, bf16[128,512]{1,0:T(8,128)(2,1)}, u32[]{:S(2)}) copy-start(bf16[128,512]{1,0:T(8,128)(2,1)} %param.13) | copy-start | bytes 393220
  6.5 10.8 %copy-start.7 = (f32[128]{0:T(128)S(1)}, f32[128]{0:T(128)}, u32[]{:S(2)}) copy-start(f32[128]{0:T(128)} %param.11) | copy-start | bytes 1540
  6.5 10.8 %copy-start.6 = (f32[128]{0:T(128)S(1)}, f32[128]{0:T(128)}, u32[]{:S(2)}) copy-start(f32[128]{0:T(128)} %param.12) | copy-start | bytes 1540
  6.5 159.7 %all-gather.5.cloned.1.call-start = ((), (), s32[]{:S(2)}) async-start(), calls=%async_computation.2 | async-start | bytes 20971520 | tf_op jit(solution)/shard_map/all_gather | solution.py:42
  6.6 10.8 %copy-start.3 = (bf16[128,128,128]{2,1,0:T(8,128)(2,1)S(1)}, bf16[128,128,128]{2,1,0:T(8,128)(2,1)}, u32[]{:S(2)}) copy-start(bf16[128,128,128]{2,1,0:T(8,128)(2,1)} %param.9) | copy-start | bytes 12582916
  22.3 13.2 %copy-start.4 = (bf16[128,128,128]{2,1,0:T(8,128)(2,1)}, bf16[128,128,128]{2,1,0:T(8,128)(2,1)S(1)}, u32[]{:S(2)}) copy-start(bf16[128,128,128]{2,1,0:T(8,128)(2,1)S(1)} %fusion.8) | copy-start | bytes 12582916
  57.5 705.3 %all-gather.3.cloned.1.call-start = ((), (), s32[]{:S(2)}) async-start(), calls=%async_computation.1 | async-start | bytes 20971520 | tf_op jit(solution)/shard_map/all_gather | solution.py:46
  58.2 115.3 %copy-start.10 = (bf16[128,128]{1,0:T(8,128)(2,1)S(1)}, bf16[128,128]{1,0:T(8,128)(2,1)}, u32[]{:S(2)}) copy-start(bf16[128,128]{1,0:T(8,128)(2,1)} %param.14) | copy-start | bytes 98308
  166.2 640.3 %all-to-all-start = ((bf16[128,512,128]{2,0,1:T(8,128)(2,1)}), bf16[128,512,128]{2,0,1:T(8,128)(2,1)}, u32[]{:S(2)}, u32[]{:S(2)}) async-start(bf16[128,512,128]{2,0,1:T(8,128)(2,1)} %all-gather.5.cloned.1.call-done), calls=%async_computation | async-start | bytes 33554432 | tf_op jit(solution)/shard_map/all_to_all | solution.py:43
  869.8 5.8 copy-start.2
  869.8 5.8 copy-start.8
  869.8 5.8 copy-start.9
  874.2 3.3 copy-start.5
  877.6 14.4 %copy-start.1 = (bf16[128,512]{1,0:T(8,128)(2,1)S(1)}, bf16[128,512]{1,0:T(8,128)(2,1)}, u32[]{:S(2)}) copy-start(bf16[128,512]{1,0:T(8,128)(2,1)} %param.13) | copy-start | bytes 393220
Sparse Core Ops, SparseCore 0:
  57.6 108.6 all-gather.4
  167.8 594.9 all-gather.2
where the time goes:
time: 900 us; the launch traced here: 899 us
  waiting for transfers between devices  709 us (79%)
  local copies, waits for them, and re-layouts  78 us (9%)
  matrix products  52.9 us (6%)
  other arithmetic  36.9 us (4%)
  between operations  14.4 us (2%)
    all_gather x1, waiting for transfers between devices, body(): lax.all_gather(left_major, 'gy', axis=2, tiled=True)  580 us
    all_gather x1, waiting for transfers between devices, body(): column_rows = lax.all_gather(right_major, ('gx', 'gz'), axis=1, tiled=True)  108 us
    all_to_all x2, local copies, waits for them, and re-layouts, body(): lax.all_to_all(column_rows, 'gy', split_axis=1, concat_axis=2, tiled=True)  46.9 us
    all_gather x1, local copies, waits for them, and re-layouts, body(): lax.all_gather(left_major, 'gy', axis=2, tiled=True)  23.4 us
    all_to_all x1, waiting for transfers between devices, body(): lax.all_to_all(column_rows, 'gy', split_axis=1, concat_axis=2, tiled=True)  20.3 us
  transfers between devices with their start and end apart: 3, of which 3 were waited for; matrix products, arithmetic and copies ran while one was open for 4% of the time, Pallas kernels for 0%

commit v1 on v0

--- a/solution.py
+++ b/solution.py
@@ -41,12 +41,38 @@
     right_major = jnp.transpose(right, (2, 0, 1))
     column_rows = lax.all_gather(right_major, ("gx", "gz"), axis=1, tiled=True)
     right_mine = lax.all_to_all(column_rows, "gy", split_axis=1, concat_axis=2, tiled=True)
-    triangle = jnp.einsum(
+    size, index, span = (lax.axis_size("gy"), lax.axis_index("gy"), left_major.shape[2])
+    right_2 = [(i, (i + 1) % size) for i in range(size)]
+    left_2 = [(i, (i - 1) % size) for i in range(size)]
+    half = size // 2
+    from_left = from_right = left_major
+    subtotal = jnp.einsum(
         "cik,cjk->cij",
-        lax.all_gather(left_major, "gy", axis=2, tiled=True),
-        right_mine,
+        left_major,
+        lax.dynamic_slice_in_dim(right_mine, index * span, left_major.shape[2], axis=2),
         preferred_element_type=jnp.float32,
     )
+    for lap in range(1, half + 1):
+        from_left = lax.ppermute(from_left, "gy", right_2)
+        if lap < size - half:
+            from_right = lax.ppermute(from_right, "gy", left_2)
+            subtotal = subtotal + jnp.einsum(
+                "cik,cjk->cij",
+                from_right,
+                lax.dynamic_slice_in_dim(
+                    right_mine, (index + lap) % size * span, from_right.shape[2], axis=2
+                ),
+                preferred_element_type=jnp.float32,
+            )
+        subtotal = subtotal + jnp.einsum(
+            "cik,cjk->cij",
+            from_left,
+            lax.dynamic_slice_in_dim(
+                right_mine, (index - lap) % size * span, from_left.shape[2], axis=2
+            ),
+            preferred_element_type=jnp.float32,
+        )
+    triangle = subtotal
     tri_norm = channel_norm(triangle, out_gain, out_bias).astype(jnp.bfloat16)
     gate = jax.nn.sigmoid(jnp.dot(flat, w_gate, preferred_element_type=jnp.float32)).reshape(
         tile_rows, tile_cols, width

time: 900 us -> 937 us (1.041)
  starting transfers between devices: 7.32 us -> 188 us
  waiting for transfers between devices: 709 us -> 532 us
  matrix products: 52.9 us -> 77.2 us
    all_gather x1 -> x0, waiting for transfers between devices: 580 us -> none  [body(): lax.all_gather(left_major, 'gy', axis=2, tiled=True)]
    ppermute x0 -> x3, waiting for transfers between devices: none -> 423 us  [the longest x2 423 us: body(): from_left = lax.ppermute(from_left, 'gy', right_2)]
    ppermute x0 -> x3, starting transfers between devices: none -> 181 us  [the longest x2 179 us: body(): from_left = lax.ppermute(from_left, 'gy', right_2)]
    dot_general x1 -> x4, matrix products: 16.4 us -> 41.9 us  [the longest x2 25.5 us: body(): jnp.einsum('cik,cjk->cij', from_left, lax.dynamic_slice_in_dim(right_mine...]
    all_gather x1 -> x0, local copies, waits for them, and re-layouts: 23.4 us -> none  [body(): lax.all_gather(left_major, 'gy', axis=2, tiled=True)]
    all_to_all x1, waiting for transfers between devices: 20.3 us -> 0.01 us  [body(): lax.all_to_all(column_rows, 'gy', split_axis=1, concat_axis=2, tiled=True)]
    ppermute x0 -> x3, local copies, waits for them, and re-layouts: none -> 20.2 us  [the longest x2 13.4 us: body(): from_left = lax.ppermute(from_left, 'gy', right_2)]
  transfers between devices with their start and end apart: 3 -> 5, of which waited for: 3 -> 3; matrix products, arithmetic and copies ran while one was open for 4% -> 4% of each run, Pallas kernels for 0% -> 0%
where the time goes in v1:
time: 937 us; the launch traced here: 929 us
  waiting for transfers between devices  532 us (57%)
  starting transfers between devices  188 us (20%)
  local copies, waits for them, and re-layouts  81.6 us (9%)
  matrix products  77.2 us (8%)
  other arithmetic  36.7 us (4%)
  between operations  14.4 us (2%)
    ppermute x2, waiting for transfers between devices, body(): from_left = lax.ppermute(from_left, 'gy', right_2)  423 us
    ppermute x2, starting transfers between devices, body(): from_left = lax.ppermute(from_left, 'gy', right_2)  179 us
    all_gather x1, waiting for transfers between devices, body(): column_rows = lax.all_gather(right_major, ('gx', 'gz'), axis=1, tiled=True)  109 us
    all_to_all x2, local copies, waits for them, and re-layouts, body(): lax.all_to_all(column_rows, 'gy', split_axis=1, concat_axis=2, tiled=True)  46.9 us
    dot_general x2, matrix products, body(): jnp.einsum('cik,cjk->cij', from_left, lax.dynamic_slice_in_dim(right_mine...  25.5 us
  transfers between devices with their start and end apart: 5, of which 3 were waited for; matrix products, arithmetic and copies ran while one was open for 4% of the time, Pallas kernels for 0%

profile of v1, /device:TPU:0, one launch (start us, length us, event | category | flops | bytes accessed | tf_op | source)
XLA Modules:
  0.0 929.4 jit_solution(4321652877712087150)
XLA Ops:
  6.5 0.0 copy-start
  6.5 0.0 copy-start.9
  6.5 0.0 copy-start.8
  6.5 0.0 all-gather.2.cloned.1.call-start
  6.6 0.0 copy-start.4
  7.4 3.8 convert_reduce_fusion
  11.2 6.0 fusion.5
  17.2 0.1 broadcast_multiply_fusion
  17.3 0.0 copy-done.9
  17.3 0.0 copy-done.8
  17.4 0.0 copy-done.4
  17.4 4.9 fusion.8
  22.3 0.0 copy-done
  22.3 0.0 copy-start.5
  22.3 13.1 %fusion.35 = f32[128,128,512]{2,1,0:T(8,128)} fusion(bf16[128,128,128]{2,1,0:T(8,128)(2,1)S(1)} %fusion.8, bf16[128,512]{1,0:T(8,128)(2,1)S(1)} %copy-done), kind=kOutput, calls=%fused_computation.43 | convolution fusion | flops 2147483648 | bytes 37879808 | tf_op jit(solution)/shard_map/dot_general | solution.py:28
  35.5 0.0 copy-done.5
  35.5 15.4 %fusion.30 = (bf16[128,128,128]{0,2,1:T(8,128)(2,1)}, bf16[128,128,128]{0,2,1:T(8,128)(2,1)}) fusion(f32[128,128,512]{2,1,0:T(8,128)} %fusion.35, f32[128,128]{1,0:T(8,128)S(1)} %broadcast_multiply_fusion), kind=kLoop, calls=%fused_computation.42 | loop fusion | flops 25165824 | bytes 42008576 | tf_op jit(solution)/shard_map/transpose | solution.py:41
  50.9 6.4 copy.16
  57.3 0.0 all-gather.2.cloned.1.call-update
  57.3 108.8 %all-gather.2.cloned.1.call-done = bf16[128,512,128]{2,0,1:T(8,128)(2,1)} async-done(((bf16[128,128,128]{2,0,1:T(8,128)(2,1)}), bf16[128,512,128]{2,0,1:T(8,128)(2,1)}) %all-gather.2.cloned.1.call-update) | async-done | bytes 16777232 | tf_op jit(solution)/shard_map/all_gather | solution.py:42
  166.1 7.0 all-to-all-start
  173.1 0.0 copy-start.12
  173.1 2.0 collective-permute-start.1
  175.1 1.9 collective-permute-start
  177.0 361.4 %collective-permute-done.1 = bf16[128,128,128]{0,2,1:T(8,128)(2,1)} collective-permute-done((bf16[128,128,128]{0,2,1:T(8,128)(2,1)}, bf16[128,128,128]{0,2,1:T(8,128)(2,1)}, u32[]{:S(2)}, u32[]{:S(2)}) %collective-permute-start.1) | collective-permute-done | bytes 4194336 | tf_op jit(solution)/shard_map/ppermute | solution.py:56
  538.3 176.7 %collective-permute-start.2 = (bf16[128,128,128]{0,2,1:T(8,128)(2,1)}, bf16[128,128,128]{0,2,1:T(8,128)(2,1)}, u32[]{:S(2)}, u32[]{:S(2)}) collective-permute-start(bf16[128,128,128]{0,2,1:T(8,128)(2,1)} %collective-permute-done.1), channel_id=1, source_target_pairs={{0,4},{4,8},{8,12},{12,0},{1,5},{5,9},{9,13},{13,1},{2,6},{6,10},{... | collective-permute-start | bytes 12582920 | tf_op jit(solution)/shard_map/ppermute | solution.py:56
  715.0 6.7 copy.18
  721.8 0.0 copy-done.12
  721.8 7.8 fusion.2
  729.5 6.7 copy.20
  736.2 0.0 collective-permute-done
  736.2 6.8 copy.19
  743.0 61.7 %collective-permute-done.2 = bf16[128,128,128]{0,2,1:T(8,128)(2,1)} collective-permute-done((bf16[128,128,128]{0,2,1:T(8,128)(2,1)}, bf16[128,128,128]{0,2,1:T(8,128)(2,1)}, u32[]{:S(2)}, u32[]{:S(2)}) %collective-permute-start.2) | collective-permute-done | bytes 4194336 | tf_op jit(solution)/shard_map/ppermute | solution.py:56
  804.7 6.7 copy.21
  811.5 0.0 all-to-all-done
  811.5 22.0 %copy.28 = bf16[128,4,128,128]{3,1,2,0:T(4,128)(2,1)} copy(bf16[128,4,128,128]{3,0,2,1:T(8,128)(2,1)} %bitcast.6) | data formatting | bytes 33554432 | tf_op jit(solution)/shard_map/all_to_all | solution.py:43
  833.5 24.9 %all_to_all.16 = bf16[128,128,512]{2,1,0:T(8,128)(2,1)} reshape(bf16[128,128,4,128]{3,2,1,0:T(4,128)(2,1)} %bitcast.25) | data formatting | bytes 33554432 | tf_op jit(solution)/shard_map/all_to_all | solution.py:43
  858.4 0.0 copy-start.3
  858.4 10.1 %fusion.25 = f32[128,128,128]{2,1,0:T(8,128)} fusion(bf16[128,128,128]{2,1,0:T(8,128)(2,1)} %copy.19, bf16[128,128,512]{2,1,0:T(8,128)(2,1)} %all_to_all.16, s32[]{:T(128)S(6)} %select_n.29), kind=kOutput, calls=%fused_computation.37 | convolution fusion | flops 536870912 | bytes 16777220 | tf_op jit(solution)/shard_map/cik,cjk->cij/dot_general | solution.py:59
  868.6 0.0 copy-done.3
  868.6 0.0 copy-start.6
  868.6 8.6 fusion.23
  877.2 0.0 copy-done.6
  877.2 6.2 fusion.27
  883.5 16.9 %fusion.42 = (f32[128,128]{1,0:T(8,128)S(1)}, f32[128,128,128]{2,1,0:T(8,128)}) fusion(bf16[128,128,128]{2,1,0:T(8,128)(2,1)} %copy.21, bf16[128,128,512]{2,1,0:T(8,128)(2,1)} %all_to_all.16, s32[]{:T(128)S(6)} %select_n.33, f32[128,128,128]{2,1,0:T(8,128)} %fusion.23, f32[128,128,128]{2,1,0:T(8,128)} %fusion.27, f32[128,128,128]{2,1,0:T(8,128)} %fusion.25), kind=kOutput, calls=%fused_computation.57 | convolution fusion | flops 545243136 | bytes 42008580 | tf_op jit(solution)/shard_map/cik,cjk->cij/dot_general | solution.py:67
  900.3 0.0 copy-start.2
  900.3 0.0 copy-start.10
  900.3 0.0 copy-start.11
  900.3 4.4 multiply_reduce_fusion
  904.8 0.0 copy-start.7
  904.8 1.3 copy-done.2
  906.1 0.0 copy-done.10
  906.1 0.0 copy-done.11
  906.1 2.0 add_convert_fusion
  908.1 0.0 copy-start.1
  908.1 0.0 copy-done.7
  908.1 14.4 %multiply_convert_fusion = bf16[128,128,128]{2,1,0:T(8,128)(2,1)} fusion(f32[128,128,128]{2,1,0:T(8,128)} %bitcast.27, bf16[128,128,128]{2,1,0:T(8,128)(2,1)S(1)} %add_convert_fusion, bf16[128,128]{1,0:T(8,128)(2,1)S(1)} %copy-done.7), kind=kOutput, calls=%fused_computation.27 | convolution fusion | flops 541065216 | bytes 16809984 | tf_op jit(solution)/shard_map/cij,cd->ijd/dot_general | solution.py:80
  922.5 0.0 copy-done.1
  (5 shorter events, 0.1 us)
Async XLA Ops:
  6.5 15.8 %copy-start = (bf16[128,512]{1,0:T(8,128)(2,1)S(1)}, bf16[128,512]{1,0:T(8,128)(2,1)}, u32[]{:S(2)}) copy-start(bf16[128,512]{1,0:T(8,128)(2,1)} %param.13) | copy-start | bytes 393220
  6.5 10.8 %copy-start.9 = (f32[128]{0:T(128)S(1)}, f32[128]{0:T(128)}, u32[]{:S(2)}) copy-start(f32[128]{0:T(128)} %param.11) | copy-start | bytes 1540
  6.5 10.8 %copy-start.8 = (f32[128]{0:T(128)S(1)}, f32[128]{0:T(128)}, u32[]{:S(2)}) copy-start(f32[128]{0:T(128)} %param.12) | copy-start | bytes 1540
  6.5 159.6 %all-gather.2.cloned.1.call-start = ((), (), s32[]{:S(2)}) async-start(), calls=%async_computation.1 | async-start | bytes 20971520 | tf_op jit(solution)/shard_map/all_gather | solution.py:42
  6.6 10.8 %copy-start.4 = (bf16[128,128,128]{2,1,0:T(8,128)(2,1)S(1)}, bf16[128,128,128]{2,1,0:T(8,128)(2,1)}, u32[]{:S(2)}) copy-start(bf16[128,128,128]{2,1,0:T(8,128)(2,1)} %param.9) | copy-start | bytes 12582916
  22.3 13.2 %copy-start.5 = (bf16[128,128,128]{2,1,0:T(8,128)(2,1)}, bf16[128,128,128]{2,1,0:T(8,128)(2,1)S(1)}, u32[]{:S(2)}) copy-start(bf16[128,128,128]{2,1,0:T(8,128)(2,1)S(1)} %fusion.8) | copy-start | bytes 12582916
  166.1 645.4 %all-to-all-start = ((bf16[128,512,128]{2,0,1:T(8,128)(2,1)}), bf16[128,512,128]{2,0,1:T(8,128)(2,1)}, u32[]{:S(2)}, u32[]{:S(2)}) async-start(bf16[128,512,128]{2,0,1:T(8,128)(2,1)} %all-gather.2.cloned.1.call-done), calls=%async_computation | async-start | bytes 33554432 | tf_op jit(solution)/shard_map/all_to_all | solution.py:43
  173.1 548.7 %copy-start.12 = (bf16[128,128]{1,0:T(8,128)(2,1)S(1)}, bf16[128,128]{1,0:T(8,128)(2,1)}, u32[]{:S(2)}) copy-start(bf16[128,128]{1,0:T(8,128)(2,1)} %param.14) | copy-start | bytes 98308
  173.1 365.2 %collective-permute-start.1 = (bf16[128,128,128]{0,2,1:T(8,128)(2,1)}, bf16[128,128,128]{0,2,1:T(8,128)(2,1)}, u32[]{:S(2)}, u32[]{:S(2)}) collective-permute-start(bf16[128,128,128]{0,2,1:T(8,128)(2,1)} %get-tuple-element.6), channel_id=1, source_target_pairs={{0,4},{4,8},{8,12},{12,0},{1,5},{5,9},{9,13},{13,1},{2,6},{6,10},{... | collective-permute-start | bytes 12582920 | tf_op jit(solution)/shard_map/ppermute | solution.py:56
  175.1 561.2 %collective-permute-start = (bf16[128,128,128]{0,2,1:T(8,128)(2,1)}, bf16[128,128,128]{0,2,1:T(8,128)(2,1)}, u32[]{:S(2)}, u32[]{:S(2)}) collective-permute-start(bf16[128,128,128]{0,2,1:T(8,128)(2,1)} %get-tuple-element.6), channel_id=1, source_target_pairs={{0,12},{4,0},{8,4},{12,8},{1,13},{5,1},{9,5},{13,9},{2,14},{6,2},{... | collective-permute-start | bytes 12582920 | tf_op jit(solution)/shard_map/ppermute | solution.py:58
  538.3 266.4 %collective-permute-start.2 = (bf16[128,128,128]{0,2,1:T(8,128)(2,1)}, bf16[128,128,128]{0,2,1:T(8,128)(2,1)}, u32[]{:S(2)}, u32[]{:S(2)}) collective-permute-start(bf16[128,128,128]{0,2,1:T(8,128)(2,1)} %collective-permute-done.1), channel_id=1, source_target_pairs={{0,4},{4,8},{8,12},{12,0},{1,5},{5,9},{9,13},{13,1},{2,6},{6,10},{... | collective-permute-start | bytes 12582920 | tf_op jit(solution)/shard_map/ppermute | solution.py:56
  858.4 10.1 %copy-start.3 = (bf16[128,128,512]{2,1,0:T(8,128)(2,1)S(1)}, bf16[128,128,512]{2,1,0:T(8,128)(2,1)}, u32[]{:S(2)}) copy-start(bf16[128,128,512]{2,1,0:T(8,128)(2,1)} %all_to_all.16) | copy-start | bytes 50331652
  868.6 8.7 copy-start.6
  900.3 5.8 copy-start.2
  900.3 5.8 copy-start.10
  900.3 5.8 copy-start.11
  904.8 3.4 copy-start.7
  908.1 14.4 %copy-start.1 = (bf16[128,512]{1,0:T(8,128)(2,1)S(1)}, bf16[128,512]{1,0:T(8,128)(2,1)}, u32[]{:S(2)}) copy-start(bf16[128,512]{1,0:T(8,128)(2,1)} %param.13) | copy-start | bytes 393220
Sparse Core Ops, SparseCore 0:
  57.4 108.6 all-gather.1
